TPU v7x, 256 devices: a whole 4x4x8 slice. The times are simulated.
256 devices in a mesh: grp: 4 (over y), dev: 64 (over x, z, core).
Axes of the slice: x: 4, y: 4, z: 8, core: 2. Of those that a mesh axis runs over, the one named last changes fastest.
Arguments:
- pool_rows: bfloat16 [262144, 1024], P(('grp', 'dev')), may hold values from -6 to 6
- sample_index: int32 [262144], P(('grp', 'dev')), may hold values from 0 to 262143, as said below
- cluster_id: int32 [262144], P(('grp', 'dev')), may hold values from 0 to 511, as said below
- child_id: int32 [262144], P(('grp', 'dev')), may hold values from 0 to 7
- old_centroids: float32 [512, 8, 1024], P('dev'), may hold values from -6 to 6
Outputs:
- centroids: float32 [512, 8, 1024], P('dev')
- child_counts: int32 [512, 8], P('dev')
Inputs may be any that keep to these rules, and one draw needn't show every extreme that they name: Sample i takes a pool row of its own aligned block of 1024 rows: sample_index[i] // 1024 == i // 1024. `cluster_id`: in each aligned block of 1024 samples (the rows of one device) the 2 clusters o * 2 to o * 2 + 1 of any owner o are named at most 8 times together, and one cluster, the same in every block, is named exactly 8 times in every block.
All inputs are finite; a program needn't handle non-finite values.
Results may differ from a plain program's by a relative error of at most 0.0003.
Values may be sent and summed in bfloat16 or wider, within the bound.
A program may use at most 64 MiB of HBM per device.

v0:
```python
import math
import jax
import jax.numpy as jnp
from jax import lax
from jax.sharding import PartitionSpec as P


def side_by_side(arrays, axis, dim, along):
    widths = [math.prod(a.shape[along:]) for a in arrays]
    both = jnp.concatenate(
        [a.reshape(*a.shape[:along], w) for a, w in zip(arrays, widths)], axis=along
    )
    filled = lax.all_gather(both, axis, axis=dim, tiled=True)
    parts = jnp.split(filled, [sum(widths[:k]) for k in range(1, len(widths))], axis=along)
    return tuple(
        (b.reshape(*filled.shape[:along], *a.shape[along:]) for a, b in zip(arrays, parts))
    )


def segment_totals(rows, segment, segments):
    onehot = (jnp.arange(segments, dtype=jnp.int32)[:, None] == segment[None, :]).astype(
        jnp.bfloat16
    )
    sums = jnp.dot(onehot, rows, preferred_element_type=jnp.float32)
    counts = jnp.sum(onehot.astype(jnp.float32), axis=1)
    return (sums, counts)


def rank_within(keys_here):
    positions = jnp.arange(keys_here.shape[0], dtype=jnp.int32)
    matches = keys_here[:, None] == keys_here[None, :]
    earlier = positions[None, :] < positions[:, None]
    return jnp.sum(matches & earlier, axis=1)


def per_device(pool_rows, sample_index, cluster_id, child_id, old_centroids):
    rows_dev, row_width = pool_rows.shape
    block_clusters, kinds = (old_centroids.shape[0], old_centroids.shape[1])
    groups = lax.axis_size("grp")
    owners = lax.axis_size("dev")
    owned = block_clusters // groups
    clusters = block_clusters * owners
    most = 4 * rows_dev // clusters
    sample = pool_rows[sample_index % rows_dev]
    holder_table = cluster_id // owned
    slot_of = holder_table * most + rank_within(holder_table)
    total_slots = clusters // owned * most
    label_of = cluster_id % owned * kinds + child_id
    buffer = jnp.zeros((total_slots, row_width), jnp.bfloat16).at[slot_of].set(sample)
    labels = jnp.full((total_slots,), -1, jnp.int32).at[slot_of].set(label_of)
    shaped = buffer.reshape(owners, groups, most, row_width)
    shaped_labels = labels.reshape(owners, groups, most)
    arrived, arrived_labels = (
        lax.all_to_all(
            lax.all_to_all(shaped, "dev", split_axis=0, concat_axis=0, tiled=True),
            "grp",
            split_axis=1,
            concat_axis=1,
            tiled=True,
        ),
        lax.all_to_all(
            lax.all_to_all(shaped_labels, "dev", split_axis=0, concat_axis=0, tiled=True),
            "grp",
            split_axis=1,
            concat_axis=1,
            tiled=True,
        ),
    )
    sums, counts = segment_totals(
        arrived.reshape(-1, row_width), arrived_labels.reshape(-1), owned * kinds
    )
    group_index = lax.axis_index("grp")
    mine = lax.dynamic_slice_in_dim(old_centroids, group_index * owned, owned, 0)
    counts_owned = counts.reshape(owned, kinds)
    fresh = (sums.reshape(owned, kinds, row_width) + mine) / (counts_owned[:, :, None] + 1.0)
    centroids, new_counts = side_by_side((fresh, counts_owned), "grp", 0, 2)
    return (centroids, new_counts.astype(jnp.int32))


def solution(mesh):
    placed = (
        P(("grp", "dev"), None),
        P(("grp", "dev")),
        P(("grp", "dev")),
        P(("grp", "dev")),
        P("dev", None, None),
    )
    return jax.shard_map(
        per_device,
        mesh=mesh,
        in_specs=placed,
        out_specs=(P("dev", None, None), P("dev", None)),
        check_vma=False,
    )
```

profile of v0, /device:TPU:2, one launch (start us, length us, event | category | flops | bytes accessed | tf_op | source)
XLA Modules:
  0.0 222.8 jit_solution(11543515831146436987)
XLA Ops:
  0.6 0.8 add_select_fusion.2
  1.5 0.5 convert_reduce_fusion
  2.0 0.7 fusion.10
  2.8 4.3 %scatter_custom_fusion = s32[2048]{0:T(1024)S(1)} fusion(s32[1024]{0:T(1024)S(1)} %get-tuple-element.3, s32[1024]{0:T(1024)S(1)} %get-tuple-element.2, s32[]{:T(128)} %constant.47.clone.1), kind=kCustom, calls=%fused_computation.34 | custom fusion | bytes 8196 | tf_op jit(solution)/shard_map/scatter | solution.py:50
  7.1 0.8 reshape.46
  7.9 12.0 %all-to-all-start = ((s32[64,4,8]{2,1,0:T(4,128)}), s32[64,4,8]{2,1,0:T(4,128)S(1)}, u32[]{:S(2)}, u32[]{:S(2)}) async-start(s32[64,4,8]{2,1,0:T(4,128)} %reshape.46), calls=%async_computation | async-start | bytes 262144 | tf_op jit(solution)/shard_map/all_to_all | solution.py:62
  20.0 15.3 %scatter_custom_fusion.1 = bf16[2048,1024]{1,0:T(8,128)(2,1)} fusion(s32[1024]{0:T(1024)S(1)} %get-tuple-element.3, bf16[1024,1024]{1,0:T(8,128)(2,1)S(1)} %copy-done, s32[1024]{0:T(1024)S(1)} %get-tuple-element.4, bf16[]{:T(256)} %constant.52.clone.1), kind=kCustom, calls=%fused_computation.6 | custom fusion | bytes 4194306 | tf_op jit(solution)/shard_map/scatter | solution.py:49
  35.3 10.5 %all-to-all-start.2 = ((bf16[64,4,8,1024]{3,2,1,0:T(8,128)(2,1)}), bf16[64,4,8,1024]{3,2,1,0:T(8,128)(2,1)}, u32[]{:S(2)}, u32[]{:S(2)}) async-start(bf16[64,4,8,1024]{3,2,1,0:T(8,128)(2,1)} %bitcast.10), calls=%async_computation.2 | async-start | bytes 8388608 | tf_op jit(solution)/shard_map/all_to_all | solution.py:55
  45.9 0.7 reshape.85
  46.6 94.0 %all-to-all-done.2 = bf16[64,4,8,1024]{3,2,1,0:T(8,128)(2,1)} async-done(((bf16[64,4,8,1024]{3,2,1,0:T(8,128)(2,1)}), bf16[64,4,8,1024]{3,2,1,0:T(8,128)(2,1)}, u32[]{:S(2)}, u32[]{:S(2)}) %all-to-all-start.2) | async-done | bytes 4194336 | tf_op jit(solution)/shard_map/all_to_all | solution.py:55
  140.5 4.5 %all-to-all-start.1 = ((s32[4,1,512]{2,1,0:T(1,128)}), s32[4,1,512]{2,1,0:T(1,128)S(1)}, u32[]{:S(2)}, u32[]{:S(2)}) async-start(s32[4,1,512]{2,1,0:T(1,128)} %reshape.85), calls=%async_computation.1 | async-start | bytes 16384 | tf_op jit(solution)/shard_map/all_to_all | solution.py:61
  145.0 4.8 %copy.22 = bf16[64,4,8,1024]{3,2,0,1:T(8,128)(2,1)} copy(bf16[64,4,8,1024]{3,2,1,0:T(8,128)(2,1)} %all-to-all-done.2) | data formatting | bytes 8388608 | tf_op jit(solution)/shard_map/all_to_all | solution.py:55
  149.8 0.6 all-to-all-done.1
  150.3 4.9 %all-to-all-start.3 = ((bf16[64,4,8,1024]{3,2,0,1:T(8,128)(2,1)}), bf16[64,4,8,1024]{3,2,0,1:T(8,128)(2,1)}, u32[]{:S(2)}, u32[]{:S(2)}) async-start(bf16[64,4,8,1024]{3,2,0,1:T(8,128)(2,1)} %copy.22), calls=%async_computation.3 | async-start | bytes 8388608 | tf_op jit(solution)/shard_map/all_to_all | solution.py:54
  155.2 0.5 broadcast.69
  155.7 0.7 reduce
  156.6 0.2 eq.55
  156.7 0.1 convert_reduce_fusion.1
  157.1 47.7 %all-to-all-done.3 = bf16[64,4,8,1024]{3,2,0,1:T(8,128)(2,1)} async-done(((bf16[64,4,8,1024]{3,2,0,1:T(8,128)(2,1)}), bf16[64,4,8,1024]{3,2,0,1:T(8,128)(2,1)}, u32[]{:S(2)}, u32[]{:S(2)}) %all-to-all-start.3) | async-done | bytes 4194336 | tf_op jit(solution)/shard_map/all_to_all | solution.py:54
  204.7 2.6 %copy.23 = bf16[64,4,8,1024]{3,2,1,0:T(8,128)(2,1)S(1)} copy(bf16[64,4,8,1024]{3,2,0,1:T(8,128)(2,1)} %all-to-all-done.3) | data formatting | bytes 8388608 | tf_op jit(solution)/shard_map/all_to_all | solution.py:54
  207.4 1.5 fusion.4
  208.9 12.4 %all_gather.3 = f32[8,8,1025]{2,1,0:T(8,128)S(1)} all-gather(f32[2,8,1025]{2,1,0:T(8,128)S(1)} %pad_maximum_fusion), channel_id=1, replica_groups=mesh['grp'=4,'dev'=64] {'grp'}, dimensions={0}, use_global_device_ids=true | all-gather | bytes 328000 | tf_op jit(solution)/shard_map/all_gather | solution.py:13
  221.4 0.7 split.8
  222.2 0.6 convert_bitcast_fusion
  (13 shorter events, 0.6 us)
Async XLA Ops:
  0.6 19.3 %copy-start = (bf16[1024,1024]{1,0:T(8,128)(2,1)S(1)}, bf16[1024,1024]{1,0:T(8,128)(2,1)}, u32[]{:S(2)}) copy-start(bf16[1024,1024]{1,0:T(8,128)(2,1)} %param.5) | copy-start | bytes 6291460
  7.9 27.4 %all-to-all-start = ((s32[64,4,8]{2,1,0:T(4,128)}), s32[64,4,8]{2,1,0:T(4,128)S(1)}, u32[]{:S(2)}, u32[]{:S(2)}) async-start(s32[64,4,8]{2,1,0:T(4,128)} %reshape.46), calls=%async_computation | async-start | bytes 262144 | tf_op jit(solution)/shard_map/all_to_all | solution.py:62
  35.3 105.3 %all-to-all-start.2 = ((bf16[64,4,8,1024]{3,2,1,0:T(8,128)(2,1)}), bf16[64,4,8,1024]{3,2,1,0:T(8,128)(2,1)}, u32[]{:S(2)}, u32[]{:S(2)}) async-start(bf16[64,4,8,1024]{3,2,1,0:T(8,128)(2,1)} %bitcast.10), calls=%async_computation.2 | async-start | bytes 8388608 | tf_op jit(solution)/shard_map/all_to_all | solution.py:55
  140.5 9.8 %all-to-all-start.1 = ((s32[4,1,512]{2,1,0:T(1,128)}), s32[4,1,512]{2,1,0:T(1,128)S(1)}, u32[]{:S(2)}, u32[]{:S(2)}) async-start(s32[4,1,512]{2,1,0:T(1,128)} %reshape.85), calls=%async_computation.1 | async-start | bytes 16384 | tf_op jit(solution)/shard_map/all_to_all | solution.py:61
  150.3 54.4 %all-to-all-start.3 = ((bf16[64,4,8,1024]{3,2,0,1:T(8,128)(2,1)}), bf16[64,4,8,1024]{3,2,0,1:T(8,128)(2,1)}, u32[]{:S(2)}, u32[]{:S(2)}) async-start(bf16[64,4,8,1024]{3,2,0,1:T(8,128)(2,1)} %copy.22), calls=%async_computation.3 | async-start | bytes 8388608 | tf_op jit(solution)/shard_map/all_to_all | solution.py:54
where the time goes:
time: 223 us
  waiting for transfers between devices  142 us (64%)
  starting transfers between devices  31.9 us (14%)
  local copies, waits for them, and re-layouts  30.5 us (14%)
  blocking collectives  12.4 us (6%)
  other arithmetic  3.54 us (2%)
    all_to_all x1, waiting for transfers between devices, per_device(): lax.all_to_all(shaped, 'dev', split_axis=0, concat_axis=0, tiled=True)  94 us
    all_to_all x1, waiting for transfers between devices, per_device(): lax.all_to_all(lax.all_to_all(shaped, 'dev', split_axis=0, concat_axis=0,...  47.7 us
    scatter x1, local copies, waits for them, and re-layouts, per_device(): jnp.zeros((total_slots, row_width), jnp.bfloat16).at[slot_of].set(sample)  15.3 us
    all_gather x1, blocking collectives, side_by_side(): filled = lax.all_gather(both, axis, axis=dim, tiled=True)  12.4 us
    all_to_all x1, starting transfers between devices, per_device(): lax.all_to_all(shaped_labels, 'dev', split_axis=0, concat_axis=0, tiled=T...  12 us
    all_to_all x1, starting transfers between devices, per_device(): lax.all_to_all(shaped, 'dev', split_axis=0, concat_axis=0, tiled=True)  10.5 us
    all_to_all x1, starting transfers between devices, per_device(): lax.all_to_all(lax.all_to_all(shaped, 'dev', split_axis=0, concat_axis=0,...  4.86 us
    all_to_all x1, local copies, waits for them, and re-layouts, per_device(): lax.all_to_all(shaped, 'dev', split_axis=0, concat_axis=0, tiled=True)  4.75 us
  transfers between devices with their start and end apart: 4, of which 3 were waited for; matrix products, arithmetic and copies ran while one was open for 10% of the time, Pallas kernels for 0%

commit v1 on v0

--- a/solution.py
+++ b/solution.py
@@ -58,12 +58,22 @@
             concat_axis=1,
             tiled=True,
         ),
-        lax.all_to_all(
-            lax.all_to_all(shaped_labels, "dev", split_axis=0, concat_axis=0, tiled=True),
-            "grp",
-            split_axis=1,
-            concat_axis=1,
-            tiled=True,
+        jnp.concatenate(
+            lax.all_to_all(
+                jnp.stack(
+                    jnp.split(
+                        lax.all_to_all(
+                            shaped_labels, "dev", split_axis=0, concat_axis=0, tiled=True
+                        ),
+                        lax.axis_size("grp"),
+                        axis=1,
+                    )
+                ),
+                "grp",
+                0,
+                0,
+            ),
+            axis=1,
         ),
     )
     sums, counts = segment_totals(

time: 223 us -> 223 us (level)
  no operation moved by 1% of the time
where the time goes in v1:
time: 223 us
  waiting for transfers between devices  142 us (64%)
  starting transfers between devices  31.9 us (14%)
  local copies, waits for them, and re-layouts  30.8 us (14%)
  blocking collectives  12.4 us (6%)
  other arithmetic  3.54 us (2%)
    all_to_all x1, waiting for transfers between devices, per_device(): lax.all_to_all(shaped, 'dev', split_axis=0, concat_axis=0, tiled=True)  93.7 us
    all_to_all x1, waiting for transfers between devices, per_device(): lax.all_to_all(lax.all_to_all(shaped, 'dev', split_axis=0, concat_axis=0,...  47.7 us
    scatter x1, local copies, waits for them, and re-layouts, per_device(): jnp.zeros((total_slots, row_width), jnp.bfloat16).at[slot_of].set(sample)  15.3 us
    all_gather x1, blocking collectives, side_by_side(): filled = lax.all_gather(both, axis, axis=dim, tiled=True)  12.4 us
    all_to_all x1, starting transfers between devices, per_device(): lax.all_to_all(shaped_labels, 'dev', split_axis=0, concat_axis=0, tiled=T...  12 us
    all_to_all x1, starting transfers between devices, per_device(): lax.all_to_all(shaped, 'dev', split_axis=0, concat_axis=0, tiled=True)  10.5 us
    all_to_all x1, starting transfers between devices, per_device(): lax.all_to_all(lax.all_to_all(shaped, 'dev', split_axis=0, concat_axis=0,...  4.86 us
    all_to_all x1, local copies, waits for them, and re-layouts, per_device(): lax.all_to_all(shaped, 'dev', split_axis=0, concat_axis=0, tiled=True)  4.75 us
  transfers between devices with their start and end apart: 4, of which 3 were waited for; matrix products, arithmetic and copies ran while one was open for 10% of the time, Pallas kernels for 0%

profile of v1, /device:TPU:2, one launch (start us, length us, event | category | flops | bytes accessed | tf_op | source)
XLA Modules:
  0.0 222.8 jit_solution(9948262098542759407)
XLA Ops:
  0.6 0.8 add_select_fusion.2
  1.5 0.5 convert_reduce_fusion
  2.0 0.7 fusion.10
  2.8 4.3 %scatter_custom_fusion = s32[2048]{0:T(1024)S(1)} fusion(s32[1024]{0:T(1024)S(1)} %get-tuple-element.7, s32[1024]{0:T(1024)S(1)} %get-tuple-element.6, s32[]{:T(128)} %constant.47.clone.1), kind=kCustom, calls=%fused_computation.35 | custom fusion | bytes 8196 | tf_op jit(solution)/shard_map/scatter | solution.py:50
  7.1 0.8 reshape.49
  7.9 12.0 %all-to-all-start = ((s32[64,4,8]{2,1,0:T(4,128)}), s32[64,4,8]{2,1,0:T(4,128)S(1)}, u32[]{:S(2)}, u32[]{:S(2)}) async-start(s32[64,4,8]{2,1,0:T(4,128)} %reshape.49), calls=%async_computation | async-start | bytes 262144 | tf_op jit(solution)/shard_map/all_to_all | solution.py:65
  20.0 15.3 %scatter_custom_fusion.1 = bf16[2048,1024]{1,0:T(8,128)(2,1)} fusion(s32[1024]{0:T(1024)S(1)} %get-tuple-element.7, bf16[1024,1024]{1,0:T(8,128)(2,1)S(1)} %copy-done, s32[1024]{0:T(1024)S(1)} %get-tuple-element.8, bf16[]{:T(256)} %constant.52.clone.1), kind=kCustom, calls=%fused_computation.6 | custom fusion | bytes 4194306 | tf_op jit(solution)/shard_map/scatter | solution.py:49
  35.3 10.5 %all-to-all-start.2 = ((bf16[64,4,8,1024]{3,2,1,0:T(8,128)(2,1)}), bf16[64,4,8,1024]{3,2,1,0:T(8,128)(2,1)}, u32[]{:S(2)}, u32[]{:S(2)}) async-start(bf16[64,4,8,1024]{3,2,1,0:T(8,128)(2,1)} %bitcast.20), calls=%async_computation.2 | async-start | bytes 8388608 | tf_op jit(solution)/shard_map/all_to_all | solution.py:55
  46.1 0.7 reshape.89
  46.9 93.7 %all-to-all-done.2 = bf16[64,4,8,1024]{3,2,1,0:T(8,128)(2,1)} async-done(((bf16[64,4,8,1024]{3,2,1,0:T(8,128)(2,1)}), bf16[64,4,8,1024]{3,2,1,0:T(8,128)(2,1)}, u32[]{:S(2)}, u32[]{:S(2)}) %all-to-all-start.2) | async-done | bytes 4194336 | tf_op jit(solution)/shard_map/all_to_all | solution.py:55
  140.5 4.5 %all-to-all-start.1 = ((s32[4,1,512]{2,1,0:T(1,128)}), s32[4,1,512]{2,1,0:T(1,128)S(1)}, u32[]{:S(2)}, u32[]{:S(2)}) async-start(s32[4,1,512]{2,1,0:T(1,128)} %reshape.89), calls=%async_computation.1 | async-start | bytes 16384 | tf_op jit(solution)/shard_map/all_to_all | solution.py:62
  145.0 4.8 %copy.38 = bf16[64,4,8,1024]{3,2,0,1:T(8,128)(2,1)} copy(bf16[64,4,8,1024]{3,2,1,0:T(8,128)(2,1)} %all-to-all-done.2) | data formatting | bytes 8388608 | tf_op jit(solution)/shard_map/all_to_all | solution.py:55
  149.8 0.6 all-to-all-done.1
  150.3 4.9 %all-to-all-start.3 = ((bf16[64,4,8,1024]{3,2,0,1:T(8,128)(2,1)}), bf16[64,4,8,1024]{3,2,0,1:T(8,128)(2,1)}, u32[]{:S(2)}, u32[]{:S(2)}) async-start(bf16[64,4,8,1024]{3,2,0,1:T(8,128)(2,1)} %copy.38), calls=%async_computation.3 | async-start | bytes 8388608 | tf_op jit(solution)/shard_map/all_to_all | solution.py:54
  155.2 0.5 broadcast.69
  155.7 0.7 reduce
  156.6 0.2 eq.55
  156.7 0.1 convert_reduce_fusion.1
  157.1 47.7 %all-to-all-done.3 = bf16[64,4,8,1024]{3,2,0,1:T(8,128)(2,1)} async-done(((bf16[64,4,8,1024]{3,2,0,1:T(8,128)(2,1)}), bf16[64,4,8,1024]{3,2,0,1:T(8,128)(2,1)}, u32[]{:S(2)}, u32[]{:S(2)}) %all-to-all-start.3) | async-done | bytes 4194336 | tf_op jit(solution)/shard_map/all_to_all | solution.py:54
  204.7 2.6 %copy.39 = bf16[64,4,8,1024]{3,2,1,0:T(8,128)(2,1)S(1)} copy(bf16[64,4,8,1024]{3,2,0,1:T(8,128)(2,1)} %all-to-all-done.3) | data formatting | bytes 8388608 | tf_op jit(solution)/shard_map/all_to_all | solution.py:54
  207.4 1.5 fusion.4
  208.9 12.4 %all_gather.3 = f32[8,8,1025]{2,1,0:T(8,128)S(1)} all-gather(f32[2,8,1025]{2,1,0:T(8,128)S(1)} %pad_maximum_fusion), channel_id=1, replica_groups=mesh['grp'=4,'dev'=64] {'grp'}, dimensions={0}, use_global_device_ids=true | all-gather | bytes 328000 | tf_op jit(solution)/shard_map/all_gather | solution.py:13
  221.4 0.7 split.28
  222.2 0.6 convert_bitcast_fusion
  (19 shorter events, 0.9 us)
Async XLA Ops:
  0.6 19.3 %copy-start = (bf16[1024,1024]{1,0:T(8,128)(2,1)S(1)}, bf16[1024,1024]{1,0:T(8,128)(2,1)}, u32[]{:S(2)}) copy-start(bf16[1024,1024]{1,0:T(8,128)(2,1)} %param.5) | copy-start | bytes 6291460
  7.9 27.4 %all-to-all-start = ((s32[64,4,8]{2,1,0:T(4,128)}), s32[64,4,8]{2,1,0:T(4,128)S(1)}, u32[]{:S(2)}, u32[]{:S(2)}) async-start(s32[64,4,8]{2,1,0:T(4,128)} %reshape.49), calls=%async_computation | async-start | bytes 262144 | tf_op jit(solution)/shard_map/all_to_all | solution.py:65
  35.3 105.3 %all-to-all-start.2 = ((bf16[64,4,8,1024]{3,2,1,0:T(8,128)(2,1)}), bf16[64,4,8,1024]{3,2,1,0:T(8,128)(2,1)}, u32[]{:S(2)}, u32[]{:S(2)}) async-start(bf16[64,4,8,1024]{3,2,1,0:T(8,128)(2,1)} %bitcast.20), calls=%async_computation.2 | async-start | bytes 8388608 | tf_op jit(solution)/shard_map/all_to_all | solution.py:55
  140.5 9.8 %all-to-all-start.1 = ((s32[4,1,512]{2,1,0:T(1,128)}), s32[4,1,512]{2,1,0:T(1,128)S(1)}, u32[]{:S(2)}, u32[]{:S(2)}) async-start(s32[4,1,512]{2,1,0:T(1,128)} %reshape.89), calls=%async_computation.1 | async-start | bytes 16384 | tf_op jit(solution)/shard_map/all_to_all | solution.py:62
  150.3 54.4 %all-to-all-start.3 = ((bf16[64,4,8,1024]{3,2,0,1:T(8,128)(2,1)}), bf16[64,4,8,1024]{3,2,0,1:T(8,128)(2,1)}, u32[]{:S(2)}, u32[]{:S(2)}) async-start(bf16[64,4,8,1024]{3,2,0,1:T(8,128)(2,1)} %copy.38), calls=%async_computation.3 | async-start | bytes 8388608 | tf_op jit(solution)/shard_map/all_to_all | solution.py:54
